TPU v7x, 32 devices: a whole 2x2x4 slice. The times are simulated.
32 devices in a mesh: dp: 8 (over y, x, core), mp: 4 (over z).
Axes of the slice: x: 2, y: 2, z: 4, core: 2. Of those that a mesh axis runs over, the one named last changes fastest.
Arguments:
- token_ids: int32 [16], replicated, may hold values from 0 to 3071
- cache_lengths: int32 [16], P('dp'), may hold values from 1 to 512
- embedding: bfloat16 [3072, 12288], P(('dp', 'mp')), may hold values from -6 to 6
- ln_gain: float32 [12288], replicated, may hold values from 0.25 to 1.75
- query_weight: bfloat16 [12288, 6144], P('dp', 'mp'), may hold values from -0.0546875 to 0.0546875
- key_cache: bfloat16 [16, 512, 6144], P('dp', None, 'mp'), may hold values from -1000 to 1000
- value_cache: bfloat16 [16, 512, 6144], P('dp', None, 'mp'), may hold values from -6 to 6
- out_weight: bfloat16 [6144, 12288], P('mp', 'dp'), may hold values from -0.078125 to 0.078125
- final_gain: float32 [12288], replicated, may hold values from 0.25 to 1.75
Outputs:
- log_probs: float32 [16, 3072], P(None, ('dp', 'mp'))
All inputs are finite; a program needn't handle non-finite values.
Results may differ from a plain program's by a relative error of at most 0.00033.
Values may be sent and summed in bfloat16 or wider, within the bound.
A program may use at most 128 MiB of HBM per device.

v0:
```python
import jax
import jax.numpy as jnp
from jax import lax
from jax.sharding import PartitionSpec as P

HD = 128


def per_device(
    token_ids,
    cache_lengths,
    embedding,
    ln_gain,
    query_weight,
    key_cache,
    value_cache,
    out_weight,
    final_gain,
):
    voc_rows = embedding.shape[0]
    model_width = embedding.shape[1]
    vocab_start = lax.axis_index(("dp", "mp")) * voc_rows
    one_hot = (token_ids[:, None] - vocab_start == jnp.arange(voc_rows)[None, :]).astype(
        jnp.bfloat16
    )
    partial_rows = jnp.dot(one_hot, embedding, preferred_element_type=jnp.float32)
    seq_here = key_cache.shape[0]
    cache_len = key_cache.shape[1]
    cols_here = out_weight.shape[1]
    dp_index = lax.axis_index("dp")
    block_sums = lax.psum_scatter(
        partial_rows.astype(jnp.bfloat16), "dp", scatter_dimension=1, tiled=True
    )
    embedded_cols = lax.psum(block_sums, "mp").astype(jnp.float32)
    first_sum, first_sq = lax.psum(
        (jnp.sum(embedded_cols, axis=-1), jnp.sum(embedded_cols * embedded_cols, axis=-1)), "dp"
    )
    first_mean = first_sum / model_width
    first_var = first_sq / model_width - first_mean * first_mean
    ln_here = lax.dynamic_slice_in_dim(ln_gain, dp_index * cols_here, cols_here, 0)
    normed_cols = (
        ln_here * (embedded_cols - first_mean[:, None]) * lax.rsqrt(first_var[:, None] + 1e-05)
    ).astype(jnp.bfloat16)
    own_rows = lax.all_to_all(normed_cols, "dp", split_axis=0, concat_axis=1, tiled=True)
    query_sum = jnp.dot(
        own_rows,
        lax.all_gather(query_weight, "dp", axis=0, tiled=True),
        preferred_element_type=jnp.float32,
    )
    queries = (query_sum * HD ** (-0.5)).astype(jnp.bfloat16)
    heads_here = queries.shape[1] // HD
    head_query = queries.reshape(seq_here, heads_here, HD)
    key_heads = key_cache.reshape(seq_here, cache_len, heads_here, HD)
    value_heads = value_cache.reshape(seq_here, cache_len, heads_here, HD)
    scores = jnp.einsum("shd,sthd->sht", head_query, key_heads, preferred_element_type=jnp.float32)
    live_mask = jnp.arange(cache_len)[None, None, :] < cache_lengths[:, None, None]
    scores = jnp.where(live_mask, scores, jnp.float32(-1e30))
    row_top = jnp.max(scores, axis=-1, keepdims=True)
    exp_terms = jnp.exp(scores - row_top)
    weights = (exp_terms / jnp.sum(exp_terms, axis=-1, keepdims=True)).astype(jnp.bfloat16)
    attended = jnp.einsum("sht,sthd->shd", weights, value_heads, preferred_element_type=jnp.float32)
    attended = attended.astype(jnp.bfloat16).reshape(seq_here, heads_here * HD)
    every_seq = lax.all_gather(attended, "dp", axis=0, tiled=True)
    mixed_out = lax.psum(jnp.dot(every_seq, out_weight, preferred_element_type=jnp.float32), "mp")
    hidden = embedded_cols + mixed_out
    row_sum, row_sq = lax.psum((jnp.sum(hidden, axis=-1), jnp.sum(hidden * hidden, axis=-1)), "dp")
    row_mean = row_sum / model_width
    row_var = row_sq / model_width - row_mean * row_mean
    gain_here = lax.dynamic_slice_in_dim(final_gain, dp_index * cols_here, cols_here, 0)
    final_normed = (
        gain_here * (hidden - row_mean[:, None]) * lax.rsqrt(row_var[:, None] + 1e-05)
    ).astype(jnp.bfloat16)
    logits = lax.dot_general(
        lax.all_gather(final_normed, "dp", axis=1, tiled=True),
        embedding,
        (((1,), (1,)), ((), ())),
        preferred_element_type=jnp.float32,
    )
    local_top = jnp.max(logits, axis=-1)
    global_top = lax.pmax(local_top, ("dp", "mp"))
    total_exp = lax.psum(jnp.sum(jnp.exp(logits - global_top[:, None]), axis=-1), ("dp", "mp"))
    return logits - global_top[:, None] - jnp.log(total_exp)[:, None]


def solution(mesh):
    return jax.shard_map(
        per_device,
        mesh=mesh,
        in_specs=(
            P(),
            P("dp"),
            P(("dp", "mp"), None),
            P(),
            P("dp", "mp"),
            P("dp", None, "mp"),
            P("dp", None, "mp"),
            P("mp", "dp"),
            P(),
        ),
        out_specs=P(None, ("dp", "mp")),
        check_vma=False,
    )
```

profile of v0, /device:TPU:0, one launch (start us, length us, event | category | flops | bytes accessed | tf_op | source)
XLA Modules:
  0.0 406.1 jit_solution(14732259672830846114)
XLA Ops:
  6.5 0.8 broadcast_subtract_fusion
  7.3 0.9 copy-done
  8.2 1.2 convolution_convert_fusion
  11.0 36.0 %reduce-scatter.2.cloned.1.call-done = bf16[16,1536]{1,0:T(8,128)(2,1)} async-done(((bf16[16,12288]{1,0:T(8,128)(2,1)}), bf16[16,1536]{1,0:T(8,128)(2,1)}) %reduce-scatter.2.cloned.1.call-update) | async-done | bytes 49168 | tf_op jit(solution)/shard_map/reduce_scatter | solution.py:31
  47.0 19.9 %psum.49 = bf16[16,1536]{1,0:T(8,128)(2,1)S(1)} all-reduce(bf16[16,1536]{1,0:T(8,128)(2,1)} %reduce-scatter.2.cloned.1.call-done), channel_id=1, replica_groups=mesh['dp'=8,'mp'=4] {'mp'}, use_global_device_ids=true, to_apply=%region_1.0 | all-reduce | flops 24576 | bytes 98304 | tf_op jit(solution)/shard_map/psum | solution.py:34
  67.1 12.8 %all-reduce.1 = (f32[16]{0:T(128)S(1)}, f32[16]{0:T(128)S(1)}) all-reduce(f32[16]{0:T(128)S(1)} %get-tuple-element.8, f32[16]{0:T(128)S(1)} %get-tuple-element.7), channel_id=1, replica_groups=mesh['dp'=8,'mp'=4] {'dp'}, use_global_device_ids=true, to_apply=%region_5.0 | all-reduce | flops 32 | bytes 256 | tf_op jit(solution)/shard_map/psum | solution.py:35
  80.6 3.3 all-to-all-start
  84.1 4.7 %copy.14 = bf16[2,512,1536]{1,2,0:T(8,128)(2,1)} copy(bf16[2,512,1536]{2,1,0:T(8,128)(2,1)} %param.14) | data formatting | bytes 6291456 | tf_op args[5]
  88.8 4.7 %copy.15 = bf16[2,512,1536]{1,2,0:T(8,128)(2,1)} copy(bf16[2,512,1536]{2,1,0:T(8,128)(2,1)} %param.15) | data formatting | bytes 6291456 | tf_op args[6]
  93.4 135.6 %all-gather.3.cloned.1.call-done = bf16[12288,1536]{1,0:T(8,128)(2,1)} async-done(((bf16[1536,1536]{1,0:T(8,128)(2,1)}), bf16[12288,1536]{1,0:T(8,128)(2,1)}) %all-gather.3.cloned.1.call-update) | async-done | bytes 37748752 | tf_op jit(solution)/shard_map/all_gather | solution.py:47
  229.1 14.3 %fusion.2 = bf16[2,1536]{1,0:T(2,128)(2,1)S(1)} fusion(bf16[2,12288]{1,0:T(2,128)(2,1)S(1)} %bitcast.29, bf16[12288,1536]{1,0:T(8,128)(2,1)} %all-gather.3.cloned.1.call-done), kind=kOutput, calls=%fused_computation.4 | convolution fusion | flops 75503616 | bytes 37804032 | tf_op jit(solution)/shard_map/dot_general | solution.py:45
  243.4 2.4 fusion.20
  246.0 2.8 fusion.12
  248.8 9.1 %all-gather = bf16[8,2,1536]{2,1,0:T(2,128)(2,1)S(1)} all-gather(bf16[1,2,1536]{2,1,0:T(2,128)(2,1)S(1)} %reshape.56), channel_id=1, replica_groups=mesh['dp'=8,'mp'=4] {'dp'}, dimensions={0}, use_global_device_ids=true | all-gather | bytes 55296 | tf_op jit(solution)/shard_map/all_gather | solution.py:63
  258.0 3.7 fusion.21
  261.7 0.8 dynamic_slice.6
  262.5 33.8 %all-reduce.4.cloned.1.call-done = f32[16,1536]{1,0:T(8,128)} async-done(((f32[16,1536]{1,0:T(8,128)}), f32[16,1536]{1,0:T(8,128)}) %all-reduce.4.cloned.1.call-update) | async-done | bytes 98320 | tf_op jit(solution)/shard_map/psum | solution.py:64
  296.3 1.0 fusion.14
  297.3 11.8 %all-reduce = (f32[16]{0:T(128)S(1)}, f32[16]{0:T(128)S(1)}) all-reduce(f32[16]{0:T(128)S(1)} %get-tuple-element.6, f32[16]{0:T(128)S(1)} %get-tuple-element.5), channel_id=1, replica_groups=mesh['dp'=8,'mp'=4] {'dp'}, use_global_device_ids=true, to_apply=%region_12.13 | all-reduce | flops 32 | bytes 256 | tf_op jit(solution)/shard_map/psum | solution.py:66
  309.2 1.0 multiply_convert_fusion
  310.1 9.5 %all_gather.11 = bf16[16,12288]{1,0:T(8,128)(2,1)S(1)} all-gather(bf16[16,1536]{1,0:T(8,128)(2,1)S(1)} %multiply_convert_fusion), channel_id=1, replica_groups=mesh['dp'=8,'mp'=4] {'dp'}, dimensions={1}, use_global_device_ids=true | all-gather | bytes 442368 | tf_op jit(solution)/shard_map/all_gather | solution.py:74
  319.7 0.8 fusion.19
  320.5 39.2 %pmax.7 = f32[16]{0:T(128)S(1)} all-reduce(f32[16]{0:T(128)S(1)} %get-tuple-element.17), channel_id=1, replica_groups=mesh['dp'=8,'mp'=4] {'dp','mp'}, use_global_device_ids=true, to_apply=%region_14.15 | all-reduce | flops 16 | bytes 128 | tf_op jit(solution)/shard_map/pmax | solution.py:80
  359.9 39.0 %psum.55 = f32[16]{0:T(128)S(1)} all-reduce(f32[16]{0:T(128)S(1)} %exponential_reduce_fusion), channel_id=1, replica_groups=mesh['dp'=8,'mp'=4] {'dp','mp'}, use_global_device_ids=true, to_apply=%region_16.17 | all-reduce | flops 16 | bytes 128 | tf_op jit(solution)/shard_map/psum | solution.py:81
  (25 shorter events, 3.7 us)
Async XLA Ops:
  6.5 1.7 copy-start
  6.5 40.5 %reduce-scatter.2.cloned.1.call-start = ((), (), s32[]{:S(2)}) async-start(), calls=%async_computation.2 | async-start | bytes 442368 | tf_op jit(solution)/shard_map/reduce_scatter | solution.py:31
  9.5 74.5 %copy-start.1 = (s32[2]{0:T(128)S(1)}, s32[2]{0:T(128)}, u32[]{:S(2)}) copy-start(s32[2]{0:T(128)} %param.10) | copy-start | bytes 28
  9.5 219.6 %all-gather.3.cloned.1.call-start = ((), (), s32[]{:S(2)}) async-start(), calls=%async_computation.3 | async-start | bytes 42467328 | tf_op jit(solution)/shard_map/all_gather | solution.py:47
  80.6 12.9 %all-to-all-start = ((bf16[8,2,1536]{2,1,0:T(2,128)(2,1)}), bf16[8,2,1536]{2,1,0:T(2,128)(2,1)S(1)}, u32[]{:S(2)}, u32[]{:S(2)}) async-start(bf16[8,2,1536]{2,1,0:T(2,128)(2,1)} %all_to_all.14), calls=%async_computation.1 | async-start | bytes 98304 | tf_op jit(solution)/shard_map/all_to_all | solution.py:44
  83.9 212.4 %all-reduce.4.cloned.1.call-start = ((), (), s32[]{:S(2)}) async-start(), calls=%async_computation.4 | async-start | bytes 196608 | tf_op jit(solution)/shard_map/psum | solution.py:64
Sparse Core Ops, SparseCore 0:
  10.4 36.5 reduce-scatter.1
  48.9 180.1 all-gather.2
  261.8 34.4 all-reduce.3
where the time goes:
time: 407 us; the launch traced here: 406 us
  waiting for transfers between devices  206 us (51%)
  blocking collectives  141 us (35%)
  matrix products  25.2 us (6%)
  between operations  13.2 us (3%)
  local copies, waits for them, and re-layouts  12.6 us (3%)
  other arithmetic  4.18 us (1%)
    all_gather x1, waiting for transfers between devices, per_device(): lax.all_gather(query_weight, 'dp', axis=0, tiled=True)  136 us
    pmax x1, blocking collectives, per_device(): global_top = lax.pmax(local_top, ('dp', 'mp'))  39.2 us
    psum x1, blocking collectives, per_device(): lax.psum(jnp.sum(jnp.exp(logits - global_top[:, None]), axis=-1), ('dp',...  39 us
    reduce_scatter x1, waiting for transfers between devices, per_device(): lax.psum_scatter(partial_rows.astype(jnp.bfloat16), 'dp', scatter_dimensi...  36 us
    psum x1, waiting for transfers between devices, per_device(): lax.psum(jnp.dot(every_seq, out_weight, preferred_element_type=jnp.float3...  33.8 us
    psum x1, blocking collectives, per_device(): embedded_cols = lax.psum(block_sums, 'mp').astype(jnp.float32)  19.9 us
    dot_general x1, matrix products, per_device(): jnp.dot(own_rows, lax.all_gather(query_weight, 'dp', axis=0, tiled=True),...  14.3 us
    psum x1, blocking collectives, per_device(): lax.psum((jnp.sum(embedded_cols, axis=-1), jnp.sum(embedded_cols * embedd...  12.8 us
  transfers between devices with their start and end apart: 4, of which 3 were waited for; matrix products, arithmetic and copies ran while one was open for 3% of the time, Pallas kernels for 0%

commit v1 on v0

--- a/solution.py
+++ b/solution.py
@@ -1,9 +1,19 @@
+import functools
 import jax
 import jax.numpy as jnp
 from jax import lax
 from jax.sharding import PartitionSpec as P
 
 HD = 128
+
+
+def change_the_results(values, peer_axis, mesh_dim):
+    for w in (peer_axis, mesh_dim):
+        values = jax.lax.psum(values, w)
+    return values
+
+
+produce_corner = functools.partial(change_the_results, peer_axis="dp", mesh_dim="mp")
 
 
 def per_device(
@@ -78,7 +88,7 @@
     )
     local_top = jnp.max(logits, axis=-1)
     global_top = lax.pmax(local_top, ("dp", "mp"))
-    total_exp = lax.psum(jnp.sum(jnp.exp(logits - global_top[:, None]), axis=-1), ("dp", "mp"))
+    total_exp = produce_corner(jnp.sum(jnp.exp(logits - global_top[:, None]), axis=-1))
     return logits - global_top[:, None] - jnp.log(total_exp)[:, None]
 
 

time: 407 us -> 391 us (0.961)
  blocking collectives: 141 us -> 126 us
    psum x1 -> x2, blocking collectives: 39 us -> 23.1 us  [change_the_results(): values = jax.lax.psum(values, w)]
where the time goes in v1:
time: 391 us; the launch traced here: 390 us
  waiting for transfers between devices  206 us (53%)
  blocking collectives  126 us (32%)
  matrix products  25.2 us (6%)
  between operations  13.2 us (3%)
  local copies, waits for them, and re-layouts  12.6 us (3%)
  other arithmetic  4.18 us (1%)
    all_gather x1, waiting for transfers between devices, per_device(): lax.all_gather(query_weight, 'dp', axis=0, tiled=True)  136 us
    pmax x1, blocking collectives, per_device(): global_top = lax.pmax(local_top, ('dp', 'mp'))  39.2 us
    reduce_scatter x1, waiting for transfers between devices, per_device(): lax.psum_scatter(partial_rows.astype(jnp.bfloat16), 'dp', scatter_dimensi...  36 us
    psum x1, waiting for transfers between devices, per_device(): lax.psum(jnp.dot(every_seq, out_weight, preferred_element_type=jnp.float3...  33.8 us
    psum x2, blocking collectives, change_the_results(): values = jax.lax.psum(values, w)  23.1 us
    psum x1, blocking collectives, per_device(): embedded_cols = lax.psum(block_sums, 'mp').astype(jnp.float32)  19.9 us
    dot_general x1, matrix products, per_device(): jnp.dot(own_rows, lax.all_gather(query_weight, 'dp', axis=0, tiled=True),...  14.3 us
    psum x1, blocking collectives, per_device(): lax.psum((jnp.sum(embedded_cols, axis=-1), jnp.sum(embedded_cols * embedd...  12.8 us
  transfers between devices with their start and end apart: 4, of which 3 were waited for; matrix products, arithmetic and copies ran while one was open for 3% of the time, Pallas kernels for 0%

profile of v1, /device:TPU:0, one launch (start us, length us, event | category | flops | bytes accessed | tf_op | source)
XLA Modules:
  0.0 390.3 jit_solution(4034430911282069510)
XLA Ops:
  6.5 0.8 broadcast_subtract_fusion
  7.3 0.9 copy-done
  8.2 1.2 convolution_convert_fusion
  11.0 36.0 %reduce-scatter.2.cloned.1.call-done = bf16[16,1536]{1,0:T(8,128)(2,1)} async-done(((bf16[16,12288]{1,0:T(8,128)(2,1)}), bf16[16,1536]{1,0:T(8,128)(2,1)}) %reduce-scatter.2.cloned.1.call-update) | async-done | bytes 49168 | tf_op jit(solution)/shard_map/reduce_scatter | solution.py:41
  47.0 19.9 %psum.56 = bf16[16,1536]{1,0:T(8,128)(2,1)S(1)} all-reduce(bf16[16,1536]{1,0:T(8,128)(2,1)} %reduce-scatter.2.cloned.1.call-done), channel_id=1, replica_groups=mesh['dp'=8,'mp'=4] {'mp'}, use_global_device_ids=true, to_apply=%region_1.0 | all-reduce | flops 24576 | bytes 98304 | tf_op jit(solution)/shard_map/psum | solution.py:44
  67.1 12.8 %all-reduce.1 = (f32[16]{0:T(128)S(1)}, f32[16]{0:T(128)S(1)}) all-reduce(f32[16]{0:T(128)S(1)} %get-tuple-element.8, f32[16]{0:T(128)S(1)} %get-tuple-element.7), channel_id=1, replica_groups=mesh['dp'=8,'mp'=4] {'dp'}, use_global_device_ids=true, to_apply=%region_5.0 | all-reduce | flops 32 | bytes 256 | tf_op jit(solution)/shard_map/psum | solution.py:45
  80.6 3.3 all-to-all-start
  84.1 4.7 %copy.14 = bf16[2,512,1536]{1,2,0:T(8,128)(2,1)} copy(bf16[2,512,1536]{2,1,0:T(8,128)(2,1)} %param.14) | data formatting | bytes 6291456 | tf_op args[5]
  88.8 4.7 %copy.15 = bf16[2,512,1536]{1,2,0:T(8,128)(2,1)} copy(bf16[2,512,1536]{2,1,0:T(8,128)(2,1)} %param.15) | data formatting | bytes 6291456 | tf_op args[6]
  93.4 135.6 %all-gather.3.cloned.1.call-done = bf16[12288,1536]{1,0:T(8,128)(2,1)} async-done(((bf16[1536,1536]{1,0:T(8,128)(2,1)}), bf16[12288,1536]{1,0:T(8,128)(2,1)}) %all-gather.3.cloned.1.call-update) | async-done | bytes 37748752 | tf_op jit(solution)/shard_map/all_gather | solution.py:57
  229.1 14.3 %fusion.2 = bf16[2,1536]{1,0:T(2,128)(2,1)S(1)} fusion(bf16[2,12288]{1,0:T(2,128)(2,1)S(1)} %bitcast.29, bf16[12288,1536]{1,0:T(8,128)(2,1)} %all-gather.3.cloned.1.call-done), kind=kOutput, calls=%fused_computation.4 | convolution fusion | flops 75503616 | bytes 37804032 | tf_op jit(solution)/shard_map/dot_general | solution.py:55
  243.4 2.4 fusion.20
  246.0 2.8 fusion.12
  248.8 9.1 %all-gather = bf16[8,2,1536]{2,1,0:T(2,128)(2,1)S(1)} all-gather(bf16[1,2,1536]{2,1,0:T(2,128)(2,1)S(1)} %reshape.56), channel_id=1, replica_groups=mesh['dp'=8,'mp'=4] {'dp'}, dimensions={0}, use_global_device_ids=true | all-gather | bytes 55296 | tf_op jit(solution)/shard_map/all_gather | solution.py:73
  258.0 3.7 fusion.21
  262.5 33.8 %all-reduce.4.cloned.1.call-done = f32[16,1536]{1,0:T(8,128)} async-done(((f32[16,1536]{1,0:T(8,128)}), f32[16,1536]{1,0:T(8,128)}) %all-reduce.4.cloned.1.call-update) | async-done | bytes 98320 | tf_op jit(solution)/shard_map/psum | solution.py:74
  296.3 1.0 fusion.14
  297.3 11.8 %all-reduce = (f32[16]{0:T(128)S(1)}, f32[16]{0:T(128)S(1)}) all-reduce(f32[16]{0:T(128)S(1)} %get-tuple-element.6, f32[16]{0:T(128)S(1)} %get-tuple-element.5), channel_id=1, replica_groups=mesh['dp'=8,'mp'=4] {'dp'}, use_global_device_ids=true, to_apply=%region_12.13 | all-reduce | flops 32 | bytes 256 | tf_op jit(solution)/shard_map/psum | solution.py:76
  309.2 1.0 multiply_convert_fusion
  310.1 9.5 %all_gather.11 = bf16[16,12288]{1,0:T(8,128)(2,1)S(1)} all-gather(bf16[16,1536]{1,0:T(8,128)(2,1)S(1)} %multiply_convert_fusion), channel_id=1, replica_groups=mesh['dp'=8,'mp'=4] {'dp'}, dimensions={1}, use_global_device_ids=true | all-gather | bytes 442368 | tf_op jit(solution)/shard_map/all_gather | solution.py:84
  319.7 0.8 fusion.19
  320.5 39.2 %pmax.7 = f32[16]{0:T(128)S(1)} all-reduce(f32[16]{0:T(128)S(1)} %get-tuple-element.17), channel_id=1, replica_groups=mesh['dp'=8,'mp'=4] {'dp','mp'}, use_global_device_ids=true, to_apply=%region_14.15 | all-reduce | flops 16 | bytes 128 | tf_op jit(solution)/shard_map/pmax | solution.py:90
  359.9 12.7 %psum.62 = f32[16]{0:T(128)S(1)} all-reduce(f32[16]{0:T(128)S(1)} %exponential_reduce_fusion), channel_id=1, replica_groups=mesh['dp'=8,'mp'=4] {'dp'}, use_global_device_ids=true, to_apply=%region_16.17 | all-reduce | flops 16 | bytes 128 | tf_op jit(solution)/shard_map/psum | solution.py:12
  372.6 10.4 %psum.63 = f32[16]{0:T(128)S(1)} all-reduce(f32[16]{0:T(128)S(1)} %psum.62), channel_id=1, replica_groups=mesh['dp'=8,'mp'=4] {'mp'}, use_global_device_ids=true, to_apply=%region_17.18 | all-reduce | flops 16 | bytes 128 | tf_op jit(solution)/shard_map/psum | solution.py:12
  (26 shorter events, 4.5 us)
Async XLA Ops:
  6.5 1.7 copy-start
  6.5 40.5 %reduce-scatter.2.cloned.1.call-start = ((), (), s32[]{:S(2)}) async-start(), calls=%async_computation.2 | async-start | bytes 442368 | tf_op jit(solution)/shard_map/reduce_scatter | solution.py:41
  9.5 74.5 %copy-start.1 = (s32[2]{0:T(128)S(1)}, s32[2]{0:T(128)}, u32[]{:S(2)}) copy-start(s32[2]{0:T(128)} %param.10) | copy-start | bytes 28
  9.5 219.6 %all-gather.3.cloned.1.call-start = ((), (), s32[]{:S(2)}) async-start(), calls=%async_computation.3 | async-start | bytes 42467328 | tf_op jit(solution)/shard_map/all_gather | solution.py:57
  80.6 12.9 %all-to-all-start = ((bf16[8,2,1536]{2,1,0:T(2,128)(2,1)}), bf16[8,2,1536]{2,1,0:T(2,128)(2,1)S(1)}, u32[]{:S(2)}, u32[]{:S(2)}) async-start(bf16[8,2,1536]{2,1,0:T(2,128)(2,1)} %all_to_all.14), calls=%async_computation.1 | async-start | bytes 98304 | tf_op jit(solution)/shard_map/all_to_all | solution.py:54
  83.9 212.4 %all-reduce.4.cloned.1.call-start = ((), (), s32[]{:S(2)}) async-start(), calls=%async_computation.4 | async-start | bytes 196608 | tf_op jit(solution)/shard_map/psum | solution.py:74
Sparse Core Ops, SparseCore 0:
  10.4 36.5 reduce-scatter.1
  48.9 180.1 all-gather.2
  261.8 34.4 all-reduce.3
